TPU v7x, 512 devices: a 4x2x32 block of a 4x8x32 slice. The times are simulated.
512 devices in a mesh: groups: 2 (over y), ctx: 32 (over z), rep: 4 (over x), row: 2 (over core).
Axes of the slice: x: 4, y: 2, z: 32, core: 2. Of those that a mesh axis runs over, the one named last changes fastest.
The devices are a block of a 4x8x32 slice.
Arguments:
- queries: bfloat16 [4, 128, 64, 128], P(None, ('groups', 'ctx', 'row'), 'rep'), parts along dimension 1, may hold values from -8 to 8
- new_keys: bfloat16 [4, 128, 8, 128], P(None, ('groups', 'ctx', 'row'), 'rep'), parts along dimension 1, may hold values from -4.5 to 4.5
- step_new_values: bfloat16 [4, 128, 8, 128], P(None, ('groups', 'ctx', 'row'), 'rep'), parts along dimension 1, may hold values from -6 to 6
- context_keys: bfloat16 [8, 32768, 128], P('rep', ('groups', 'ctx')), parts along dimension 1, may hold values from -6 to 6
- context_values: bfloat16 [8, 32768, 128], P('rep', ('groups', 'ctx')), parts along dimension 1, may hold values from -6 to 6
- cluster_centroid_keys: bfloat16 [8, 256, 128], P('rep', ('groups', 'ctx')), parts along dimension 1, may hold values from -4 to 4
- cluster_mean_values: bfloat16 [8, 256, 128], P('rep', ('groups', 'ctx')), parts along dimension 1, may hold values from -6 to 6
- cluster_page_slot: int32 [8, 256], P('rep', 'groups'), parts along dimension 1, may hold values from 0 to 127, each once within a row
- picks: int32 [128, 8, 16], P(('groups', 'ctx', 'row'), 'rep'), parts along dimension 0, may hold values from 0 to 127, all different within a row
Outputs:
- attention: bfloat16 [4, 128, 64, 128], P(None, ('groups', 'ctx', 'row'), 'rep'), parts along dimension 1
There are 2 independent parts, one for each index of `groups`. A program takes and returns all parts, laid end to end along the dimension named above; each array names one. Nothing has to cross between parts.
Inputs may be any that keep to these rules, and one draw needn't show every extreme that they name: `picks`: for each row and key-value head, 16 different cluster ids. `cluster_page_slot`: for each key-value head, every cluster has its own page slot; slot p lies on context shard p // 4.
All inputs are finite; a program needn't handle non-finite values.
Results may differ from a plain program's by a relative error of at most 0.0027.
Values may be sent and summed in bfloat16 or wider, within the bound.
No kernel may reach another device: no remote copies, remote signals or barrier semaphores. Data moves between devices by JAX's collectives and lax.ppermute only.
A program may use at most 64 MiB of HBM per device.

v0:
```python
import math
import jax
import jax.numpy as jnp
from jax import lax
from jax.sharding import PartitionSpec as P

FLOOR_SCORE = -10000.0


def from_everyone(x, axis):
    peers = lax.axis_size(axis)
    return lax.all_to_all(jnp.broadcast_to(x[None], (peers, *x.shape)), axis, 0, 0, tiled=True)


def laid_out(pieces, dim):
    lengths = list(pieces.shape[1:])
    lengths[dim] *= pieces.shape[0]
    return jnp.moveaxis(pieces, 0, dim).reshape(lengths)


def gather_directly(x, axis, dim):
    pieces = from_everyone(x, axis)
    return laid_out(pieces, dim)


def tail_block(queries, new_keys, step_new_values, logit_multiplier):
    num_steps, num_rows, num_heads, head_width = queries.shape
    kv_heads = new_keys.shape[2]
    grouped = queries.astype(jnp.float32).reshape(
        num_steps, num_rows, kv_heads, num_heads // kv_heads, head_width
    )
    scores = (
        jnp.einsum("srhgd,trhd->srhgt", grouped, new_keys.astype(jnp.float32)) * logit_multiplier
    )
    step_ids = jnp.arange(num_steps, dtype=jnp.int32)
    causal = (step_ids[None, :] <= step_ids[:, None])[:, None, None, None, :]
    block_top = jnp.max(jnp.where(causal, scores, FLOOR_SCORE), axis=-1)
    weights = jnp.where(causal, jnp.exp(scores - block_top[..., None]), 0.0)
    sum_total = jnp.sum(weights, axis=-1)
    rounded = weights.astype(jnp.bfloat16).astype(jnp.float32)
    tail_out = jnp.einsum("srhgt,trhd->srhgd", rounded, step_new_values.astype(jnp.float32))
    return (
        tail_out.reshape(num_steps, num_rows, num_heads, head_width),
        sum_total.reshape(num_steps, num_rows, num_heads),
        block_top.reshape(num_steps, num_rows, num_heads),
    )


def per_device(
    queries,
    new_keys,
    step_new_values,
    context_keys,
    context_values,
    cluster_centroid_keys,
    cluster_mean_values,
    cluster_page_slot,
    picks,
):
    num_steps = queries.shape[0]
    num_heads = queries.shape[2]
    head_width = queries.shape[3]
    kv_local = context_keys.shape[0]
    span_tokens = context_keys.shape[1]
    cl_local = cluster_centroid_keys.shape[1]
    grouping_member_entries = span_tokens // cl_local
    query_group_size = num_heads // kv_local
    logit_multiplier = 1.0 / math.sqrt(head_width)
    membership_log_weight = math.log(grouping_member_entries)
    shard_index = lax.axis_index("ctx")
    gathered = lax.all_gather(queries, "ctx", axis=1, tiled=True)
    chosen = gather_directly(picks, "ctx", 0)
    rows_all = gathered.shape[1]
    cluster_ids = jnp.arange(cluster_page_slot.shape[1], dtype=jnp.int32)
    pick_hits = chosen[..., None] == cluster_ids
    picked_slots = jnp.sum(jnp.where(pick_hits, cluster_page_slot[None, :, None, :], 0), axis=-1)
    local_ids = shard_index * cl_local + jnp.arange(cl_local, dtype=jnp.int32)
    slot_used = jnp.any(picked_slots[..., None] == local_ids, axis=2)
    cluster_used = jnp.any(chosen[..., None] == local_ids, axis=2)
    step_outs, step_totals, step_tops = ([], [], [])
    for step_index in range(num_steps):
        head_outs, head_totals, head_tops = ([], [], [])
        for current_head_index in range(kv_local):
            generation_probe_vectors = gathered[
                step_index,
                :,
                current_head_index * query_group_size : (current_head_index + 1) * query_group_size,
                :,
            ].reshape(rows_all * query_group_size, head_width)
            exact_mask = slot_used[:, current_head_index][:, None, :, None]
            coarse_mask = jnp.logical_not(cluster_used[:, current_head_index])[:, None, :]
            exact_scores = (
                jnp.einsum(
                    "qd,kd->qk",
                    generation_probe_vectors,
                    context_keys[current_head_index],
                    preferred_element_type=jnp.float32,
                )
                * logit_multiplier
            )
            exact_scores = exact_scores.reshape(
                rows_all, query_group_size, cl_local, grouping_member_entries
            )
            prototype_logits = (
                jnp.einsum(
                    "qd,kd->qk",
                    generation_probe_vectors,
                    cluster_centroid_keys[current_head_index],
                    preferred_element_type=jnp.float32,
                )
                * logit_multiplier
                + membership_log_weight
            )
            prototype_logits = prototype_logits.reshape(rows_all, query_group_size, cl_local)
            block_top = jnp.maximum(
                jnp.max(jnp.where(exact_mask, exact_scores, FLOOR_SCORE), axis=(2, 3)),
                jnp.max(jnp.where(coarse_mask, prototype_logits, FLOOR_SCORE), axis=2),
            )
            exact_weights = jnp.where(
                exact_mask, jnp.exp(exact_scores - block_top[:, :, None, None]), 0.0
            )
            coarse_weights = jnp.where(
                coarse_mask, jnp.exp(prototype_logits - block_top[:, :, None]), 0.0
            )
            sum_total = jnp.sum(exact_weights, axis=(2, 3)) + jnp.sum(coarse_weights, axis=2)
            block_out = jnp.dot(
                exact_weights.astype(jnp.bfloat16).reshape(
                    rows_all * query_group_size, span_tokens
                ),
                context_values[current_head_index],
                preferred_element_type=jnp.float32,
            )
            block_out = block_out + jnp.dot(
                coarse_weights.astype(jnp.bfloat16).reshape(rows_all * query_group_size, cl_local),
                cluster_mean_values[current_head_index],
                preferred_element_type=jnp.float32,
            )
            head_outs.append(block_out.reshape(rows_all, query_group_size, head_width))
            head_totals.append(sum_total)
            head_tops.append(block_top)
        step_outs.append(jnp.concatenate(head_outs, axis=1))
        step_totals.append(jnp.concatenate(head_totals, axis=1))
        step_tops.append(jnp.concatenate(head_tops, axis=1))
    partial_outs = jnp.stack(step_outs)
    partial_totals = jnp.stack(step_totals)
    partial_tops = jnp.stack(step_tops)
    got_tops, got_totals, got_outs = (
        lax.all_to_all(partial_tops[None], "ctx", split_axis=2, concat_axis=0, tiled=True),
        lax.all_to_all(partial_totals[None], "ctx", split_axis=2, concat_axis=0, tiled=True),
        lax.all_to_all(partial_outs[None], "ctx", split_axis=2, concat_axis=0, tiled=True),
    )
    best_top = jnp.max(got_tops, axis=0)
    factor = jnp.exp(got_tops - best_top)
    sum_total = jnp.sum(factor * got_totals, axis=0)
    merged = jnp.sum(factor[..., None] * got_outs, axis=0)
    tail_out, tail_total, tail_top = tail_block(
        queries, new_keys, step_new_values, logit_multiplier
    )
    overall = jnp.maximum(best_top, tail_top)
    context_factor = jnp.exp(best_top - overall)
    tail_factor = jnp.exp(tail_top - overall)
    numer = context_factor[..., None] * merged + tail_factor[..., None] * tail_out
    denom = context_factor * sum_total + tail_factor * tail_total
    return (numer / denom[..., None]).astype(jnp.bfloat16)


def solution(mesh):
    return jax.shard_map(
        per_device,
        mesh=mesh,
        in_specs=(
            P(None, ("groups", "ctx", "row"), "rep", None),
            P(None, ("groups", "ctx", "row"), "rep", None),
            P(None, ("groups", "ctx", "row"), "rep", None),
            P("rep", ("groups", "ctx"), None),
            P("rep", ("groups", "ctx"), None),
            P("rep", ("groups", "ctx"), None),
            P("rep", ("groups", "ctx"), None),
            P("rep", "groups"),
            P(("groups", "ctx", "row"), "rep", None),
        ),
        out_specs=P(None, ("groups", "ctx", "row"), "rep", None),
        check_vma=False,
    )
```

profile of v0, /device:TPU:46, one launch (start us, length us, event | category | flops | bytes accessed | tf_op | source)
XLA Modules:
  0.0 299.1 jit_solution(11759617294997700711)
XLA Ops:
  0.0 0.7 copy-done.7
  0.7 0.6 broadcast_in_dim.256
  1.3 45.9 %all-to-all-start = ((s32[32,1,2,16]{3,2,1,0:T(2,128)}), s32[32,1,2,16]{3,2,1,0:T(2,128)S(1)}, u32[]{:S(2)}, u32[]{:S(2)}) async-start(s32[32,1,2,16]{3,2,1,0:T(2,128)} %broadcast_in_dim.256), calls=%async_computation | async-start | bytes 65536 | tf_op jit(solution)/shard_map/all_to_all | solution.py:12
  47.2 59.1 %all_gather.3 = bf16[4,32,16,128]{3,2,1,0:T(8,128)(2,1)S(1)} all-gather(bf16[4,1,16,128]{3,2,1,0:T(8,128)(2,1)S(1)} %copy-done.5), channel_id=1, replica_groups=mesh['groups'=2,'ctx'=32,'rep'=4,'row'=2] {'ctx'}, dimensions={1}, use_global_device_ids=true | all-gather | bytes 540672 | tf_op jit(solution)/shard_map/all_gather | solution.py:71
  108.5 0.6 copy-done.6
  109.1 1.4 select_reduce_fusion
  111.0 1.2 fusion.22
  112.2 1.0 select_reduce_fusion.8
  113.3 0.4 fusion.48
  113.7 1.4 fusion.34
  115.8 0.7 fusion.36
  116.6 0.4 fusion.46
  117.5 1.2 fusion.18
  118.7 1.0 select_reduce_fusion.9
  119.7 0.4 fusion.56
  120.0 1.4 fusion.26
  121.5 0.4 fusion.52
  121.8 0.4 fusion.50
  122.2 0.7 fusion.28
  122.9 0.4 fusion.54
  123.7 0.6 copy-done.4
  127.3 0.7 copy.58
  128.0 17.9 %all-to-all-start.3 = ((f32[1,4,32,16]{3,1,0,2:T(4,128)}), f32[1,4,32,16]{3,1,0,2:T(4,128)S(1)}, u32[]{:S(2)}, u32[]{:S(2)}) async-start(f32[1,4,32,16]{3,1,0,2:T(4,128)} %copy.58), calls=%async_computation.3 | async-start | bytes 131072 | tf_op jit(solution)/shard_map/all_to_all | solution.py:149
  146.2 0.7 copy.52
  147.0 22.9 %all-to-all-done.3 = f32[1,4,32,16]{3,1,0,2:T(4,128)S(1)} async-done(((f32[1,4,32,16]{3,1,0,2:T(4,128)}), f32[1,4,32,16]{3,1,0,2:T(4,128)S(1)}, u32[]{:S(2)}, u32[]{:S(2)}) %all-to-all-start.3) | async-done | bytes 8224 | tf_op jit(solution)/shard_map/all_to_all | solution.py:149
  169.8 4.8 %all-to-all-start.1 = ((f32[1,4,32,16]{3,1,0,2:T(4,128)}), f32[1,4,32,16]{3,1,0,2:T(4,128)S(1)}, u32[]{:S(2)}, u32[]{:S(2)}) async-start(f32[1,4,32,16]{3,1,0,2:T(4,128)} %copy.52), calls=%async_computation.1 | async-start | bytes 131072 | tf_op jit(solution)/shard_map/all_to_all | solution.py:148
  174.6 1.1 maximum_bitcast_fusion
  175.7 22.7 %all-to-all-done.1 = f32[1,4,32,16]{3,1,0,2:T(4,128)S(1)} async-done(((f32[1,4,32,16]{3,1,0,2:T(4,128)}), f32[1,4,32,16]{3,1,0,2:T(4,128)S(1)}, u32[]{:S(2)}, u32[]{:S(2)}) %all-to-all-start.1) | async-done | bytes 8224 | tf_op jit(solution)/shard_map/all_to_all | solution.py:148
  198.4 4.8 %all-to-all-start.2 = ((f32[1,4,32,16,128]{4,3,1,0,2:T(8,128)}), f32[1,4,32,16,128]{4,3,1,0,2:T(8,128)S(1)}, u32[]{:S(2)}, u32[]{:S(2)}) async-start(f32[1,4,32,16,128]{4,3,1,0,2:T(8,128)} %maximum_bitcast_fusion), calls=%async_computation.2 | async-start | bytes 2097152 | tf_op jit(solution)/shard_map/all_to_all | solution.py:150
  203.3 0.7 copy-done.9
  204.8 93.2 %all-to-all-done.2 = f32[1,4,32,16,128]{4,3,1,0,2:T(8,128)S(1)} async-done(((f32[1,4,32,16,128]{4,3,1,0,2:T(8,128)}), f32[1,4,32,16,128]{4,3,1,0,2:T(8,128)S(1)}, u32[]{:S(2)}, u32[]{:S(2)}) %all-to-all-start.2) | async-done | bytes 1048608 | tf_op jit(solution)/shard_map/all_to_all | solution.py:150
  298.4 0.7 fusion.121
  (109 shorter events, 8.9 us)
Async XLA Ops:
  0.0 204.4 %copy-start = (bf16[4,1,2,128]{3,2,1,0:T(2,128)(2,1)S(1)}, bf16[4,1,2,128]{3,2,1,0:T(2,128)(2,1)}, u32[]{:S(2)}) copy-start(bf16[4,1,2,128]{3,2,1,0:T(2,128)(2,1)} %param.11) | copy-start | bytes 6148
  0.0 0.7 copy-start.7
  1.3 45.9 %copy-start.5 = (bf16[4,1,16,128]{3,2,1,0:T(8,128)(2,1)S(1)}, bf16[4,1,16,128]{3,2,1,0:T(8,128)(2,1)}, u32[]{:S(2)}) copy-start(bf16[4,1,16,128]{3,2,1,0:T(8,128)(2,1)} %param.9) | copy-start | bytes 49156
  1.3 107.1 %all-to-all-start = ((s32[32,1,2,16]{3,2,1,0:T(2,128)}), s32[32,1,2,16]{3,2,1,0:T(2,128)S(1)}, u32[]{:S(2)}, u32[]{:S(2)}) async-start(s32[32,1,2,16]{3,2,1,0:T(2,128)} %broadcast_in_dim.256), calls=%async_computation | async-start | bytes 65536 | tf_op jit(solution)/shard_map/all_to_all | solution.py:12
  47.2 59.1 %copy-start.8 = (bf16[2,4,128]{2,1,0:T(4,128)(2,1)S(1)}, bf16[2,4,128]{2,1,0:T(4,128)(2,1)}, u32[]{:S(2)}) copy-start(bf16[2,4,128]{2,1,0:T(4,128)(2,1)} %param.14) | copy-start | bytes 6148
  106.3 1.8 copy-start.3
  106.3 1.1 copy-start.1
  108.4 0.7 copy-start.6
  111.0 2.3 copy-start.2
  123.6 0.7 copy-start.4
  128.0 41.9 %all-to-all-start.3 = ((f32[1,4,32,16]{3,1,0,2:T(4,128)}), f32[1,4,32,16]{3,1,0,2:T(4,128)S(1)}, u32[]{:S(2)}, u32[]{:S(2)}) async-start(f32[1,4,32,16]{3,1,0,2:T(4,128)} %copy.58), calls=%async_computation.3 | async-start | bytes 131072 | tf_op jit(solution)/shard_map/all_to_all | solution.py:149
  169.8 28.5 %all-to-all-start.1 = ((f32[1,4,32,16]{3,1,0,2:T(4,128)}), f32[1,4,32,16]{3,1,0,2:T(4,128)S(1)}, u32[]{:S(2)}, u32[]{:S(2)}) async-start(f32[1,4,32,16]{3,1,0,2:T(4,128)} %copy.52), calls=%async_computation.1 | async-start | bytes 131072 | tf_op jit(solution)/shard_map/all_to_all | solution.py:148
  198.4 99.6 %all-to-all-start.2 = ((f32[1,4,32,16,128]{4,3,1,0,2:T(8,128)}), f32[1,4,32,16,128]{4,3,1,0,2:T(8,128)S(1)}, u32[]{:S(2)}, u32[]{:S(2)}) async-start(f32[1,4,32,16,128]{4,3,1,0,2:T(8,128)} %maximum_bitcast_fusion), calls=%async_computation.2 | async-start | bytes 2097152 | tf_op jit(solution)/shard_map/all_to_all | solution.py:150
  203.2 0.7 copy-start.9
where the time goes:
time: 300 us; the launch traced here: 299 us
  waiting for transfers between devices  139 us (46%)
  starting transfers between devices  73.4 us (24%)
  blocking collectives  59.1 us (20%)
  matrix products  14.1 us (5%)
  local copies, waits for them, and re-layouts  7.04 us (2%)
  other arithmetic  6.17 us (2%)
    all_to_all x1, waiting for transfers between devices, per_device(): lax.all_to_all(partial_outs[None], 'ctx', split_axis=2, concat_axis=0, ti...  93.2 us
    all_gather x1, blocking collectives, per_device(): gathered = lax.all_gather(queries, 'ctx', axis=1, tiled=True)  59.1 us
    all_to_all x1, starting transfers between devices, from_everyone(): lax.all_to_all(jnp.broadcast_to(x[None], (peers, *x.shape)), axis, 0, 0,...  45.9 us
    all_to_all x1, waiting for transfers between devices, per_device(): lax.all_to_all(partial_totals[None], 'ctx', split_axis=2, concat_axis=0,...  22.9 us
    all_to_all x1, waiting for transfers between devices, per_device(): lax.all_to_all(partial_tops[None], 'ctx', split_axis=2, concat_axis=0, ti...  22.7 us
    all_to_all x1, starting transfers between devices, per_device(): lax.all_to_all(partial_totals[None], 'ctx', split_axis=2, concat_axis=0,...  17.9 us
    dot_general x8, matrix products, per_device(): jnp.einsum('qd,kd->qk', generation_probe_vectors, context_keys[current_he...  6.08 us
  transfers between devices with their start and end apart: 4, of which 3 were waited for; matrix products, arithmetic and copies ran while one was open for 2% of the time, Pallas kernels for 0%

commit v1 on v0

--- a/solution.py
+++ b/solution.py
@@ -5,6 +5,14 @@
 from jax.sharding import PartitionSpec as P
 
 FLOOR_SCORE = -10000.0
+
+
+def gather_from_all(array, axis, dim):
+    count = lax.axis_size(axis)
+    repeats = [count if d == dim else 1 for d in range(array.ndim)]
+    return lax.all_to_all(
+        jnp.tile(array, repeats), axis, split_axis=dim, concat_axis=dim, tiled=True
+    )
 
 
 def from_everyone(x, axis):
@@ -68,7 +76,7 @@
     logit_multiplier = 1.0 / math.sqrt(head_width)
     membership_log_weight = math.log(grouping_member_entries)
     shard_index = lax.axis_index("ctx")
-    gathered = lax.all_gather(queries, "ctx", axis=1, tiled=True)
+    gathered = gather_from_all(queries, "ctx", 1)
     chosen = gather_directly(picks, "ctx", 0)
     rows_all = gathered.shape[1]
     cluster_ids = jnp.arange(cluster_page_slot.shape[1], dtype=jnp.int32)

time: 300 us -> 320 us (1.067)
  the two profiles are of different devices: /device:TPU:46 before, /device:TPU:44 now
where the time goes in v1:
time: 320 us
  waiting for transfers between devices  210 us (66%)
  blocking collectives  68.1 us (21%)
  starting transfers between devices  19.3 us (6%)
  matrix products  9.06 us (3%)
  local copies, waits for them, and re-layouts  6.86 us (2%)
  other arithmetic  6.13 us (2%)
    all_to_all x1, waiting for transfers between devices, per_device(): lax.all_to_all(partial_outs[None], 'ctx', split_axis=2, concat_axis=0, ti...  103 us
    all_to_all x1, blocking collectives, from_everyone(): lax.all_to_all(jnp.broadcast_to(x[None], (peers, *x.shape)), axis, 0, 0,...  68.1 us
    all_to_all x1, waiting for transfers between devices, gather_from_all(): lax.all_to_all(jnp.tile(array, repeats), axis, split_axis=dim, concat_axi...  61.1 us
    all_to_all x1, waiting for transfers between devices, per_device(): lax.all_to_all(partial_tops[None], 'ctx', split_axis=2, concat_axis=0, ti...  22.7 us
    all_to_all x1, waiting for transfers between devices, per_device(): lax.all_to_all(partial_totals[None], 'ctx', split_axis=2, concat_axis=0,...  22.7 us
  transfers between devices with their start and end apart: 4, of which 4 were waited for; matrix products, arithmetic and copies ran while one was open for 2% of the time, Pallas kernels for 0%

profile of v1, /device:TPU:44, one launch (start us, length us, event | category | flops | bytes accessed | tf_op | source)
XLA Modules:
  0.0 319.7 jit_solution(12295869245952611823)
XLA Ops:
  0.0 0.7 copy-done.6
  0.7 68.1 %all_to_all.67 = s32[32,1,2,16]{3,2,1,0:T(2,128)S(1)} all-to-all(s32[32,1,2,16]{3,2,1,0:T(2,128)S(1)} %broadcast_in_dim.256), channel_id=1, replica_groups=mesh['groups'=2,'ctx'=32,'rep'=4,'row'=2] {'ctx'}, dimensions={0} | all-to-all | bytes 8192 | tf_op jit(solution)/shard_map/all_to_all | solution.py:20
  68.8 0.9 tile.10
  69.7 4.9 %all-to-all-start.1 = ((bf16[4,32,16,128]{3,2,0,1:T(8,128)(2,1)}), bf16[4,32,16,128]{3,2,0,1:T(8,128)(2,1)S(1)}, u32[]{:S(2)}, u32[]{:S(2)}) async-start(bf16[4,32,16,128]{3,2,0,1:T(8,128)(2,1)} %tile.10), calls=%async_computation.1 | async-start | bytes 1048576 | tf_op jit(solution)/shard_map/all_to_all | solution.py:13
  74.7 1.4 select_reduce_fusion
  76.9 61.1 %all-to-all-done.1 = bf16[4,32,16,128]{3,2,0,1:T(8,128)(2,1)S(1)} async-done(((bf16[4,32,16,128]{3,2,0,1:T(8,128)(2,1)}), bf16[4,32,16,128]{3,2,0,1:T(8,128)(2,1)S(1)}, u32[]{:S(2)}, u32[]{:S(2)}) %all-to-all-start.1) | async-done | bytes 524320 | tf_op jit(solution)/shard_map/all_to_all | solution.py:13
  138.5 0.3 fusion.22
  139.1 0.4 copy-done.2
  139.5 0.4 fusion.48
  140.3 0.5 fusion.34
  140.9 0.4 fusion.44
  141.3 0.4 fusion.42
  141.6 0.7 fusion.36
  142.3 0.4 fusion.46
  143.9 0.4 fusion.56
  144.8 0.5 fusion.26
  145.3 0.4 fusion.52
  145.7 0.4 fusion.50
  146.1 0.7 fusion.28
  146.8 0.4 fusion.54
  147.5 0.6 copy-done.3
  151.2 0.7 copy.58
  151.8 4.8 %all-to-all-start.4 = ((f32[1,4,32,16]{3,1,0,2:T(4,128)}), f32[1,4,32,16]{3,1,0,2:T(4,128)S(1)}, u32[]{:S(2)}, u32[]{:S(2)}) async-start(f32[1,4,32,16]{3,1,0,2:T(4,128)} %copy.58), calls=%async_computation.4 | async-start | bytes 131072 | tf_op jit(solution)/shard_map/all_to_all | solution.py:157
  156.9 0.7 copy.52
  157.7 22.7 %all-to-all-done.4 = f32[1,4,32,16]{3,1,0,2:T(4,128)S(1)} async-done(((f32[1,4,32,16]{3,1,0,2:T(4,128)}), f32[1,4,32,16]{3,1,0,2:T(4,128)S(1)}, u32[]{:S(2)}, u32[]{:S(2)}) %all-to-all-start.4) | async-done | bytes 8224 | tf_op jit(solution)/shard_map/all_to_all | solution.py:157
  180.3 4.8 %all-to-all-start.2 = ((f32[1,4,32,16]{3,1,0,2:T(4,128)}), f32[1,4,32,16]{3,1,0,2:T(4,128)S(1)}, u32[]{:S(2)}, u32[]{:S(2)}) async-start(f32[1,4,32,16]{3,1,0,2:T(4,128)} %copy.52), calls=%async_computation.2 | async-start | bytes 131072 | tf_op jit(solution)/shard_map/all_to_all | solution.py:156
  185.1 1.1 maximum_bitcast_fusion
  186.2 22.7 %all-to-all-done.2 = f32[1,4,32,16]{3,1,0,2:T(4,128)S(1)} async-done(((f32[1,4,32,16]{3,1,0,2:T(4,128)}), f32[1,4,32,16]{3,1,0,2:T(4,128)S(1)}, u32[]{:S(2)}, u32[]{:S(2)}) %all-to-all-start.2) | async-done | bytes 8224 | tf_op jit(solution)/shard_map/all_to_all | solution.py:156
  208.8 4.8 %all-to-all-start.3 = ((f32[1,4,32,16,128]{4,3,1,0,2:T(8,128)}), f32[1,4,32,16,128]{4,3,1,0,2:T(8,128)S(1)}, u32[]{:S(2)}, u32[]{:S(2)}) async-start(f32[1,4,32,16,128]{4,3,1,0,2:T(8,128)} %maximum_bitcast_fusion), calls=%async_computation.3 | async-start | bytes 2097152 | tf_op jit(solution)/shard_map/all_to_all | solution.py:158
  213.7 0.7 copy-done.8
  215.3 103.4 %all-to-all-done.3 = f32[1,4,32,16,128]{4,3,1,0,2:T(8,128)S(1)} async-done(((f32[1,4,32,16,128]{4,3,1,0,2:T(8,128)}), f32[1,4,32,16,128]{4,3,1,0,2:T(8,128)S(1)}, u32[]{:S(2)}, u32[]{:S(2)}) %all-to-all-start.3) | async-done | bytes 1048608 | tf_op jit(solution)/shard_map/all_to_all | solution.py:158
  319.0 0.7 fusion.121
  (108 shorter events, 8.6 us)
Async XLA Ops:
  0.0 214.8 %copy-start = (bf16[4,1,2,128]{3,2,1,0:T(2,128)(2,1)S(1)}, bf16[4,1,2,128]{3,2,1,0:T(2,128)(2,1)}, u32[]{:S(2)}) copy-start(bf16[4,1,2,128]{3,2,1,0:T(2,128)(2,1)} %param.11) | copy-start | bytes 6148
  0.0 0.7 copy-start.6
  0.7 68.1 %copy-start.4 = (bf16[4,1,16,128]{3,2,1,0:T(8,128)(2,1)S(1)}, bf16[4,1,16,128]{3,2,1,0:T(8,128)(2,1)}, u32[]{:S(2)}) copy-start(bf16[4,1,16,128]{3,2,1,0:T(8,128)(2,1)} %param.9) | copy-start | bytes 49156
  69.7 5.0 %copy-start.5 = (s32[2,128]{1,0:T(2,128)S(1)}, s32[2,128]{1,0:T(2,128)}, u32[]{:S(2)}) copy-start(s32[2,128]{1,0:T(2,128)} %param.16) | copy-start | bytes 3076
  69.7 68.4 %all-to-all-start.1 = ((bf16[4,32,16,128]{3,2,0,1:T(8,128)(2,1)}), bf16[4,32,16,128]{3,2,0,1:T(8,128)(2,1)S(1)}, u32[]{:S(2)}, u32[]{:S(2)}) async-start(bf16[4,32,16,128]{3,2,0,1:T(8,128)(2,1)} %tile.10), calls=%async_computation.1 | async-start | bytes 1048576 | tf_op jit(solution)/shard_map/all_to_all | solution.py:13
  74.7 63.9 %copy-start.1 = (bf16[2,512,128]{2,1,0:T(8,128)(2,1)S(1)}, bf16[2,512,128]{2,1,0:T(8,128)(2,1)}, u32[]{:S(2)}) copy-start(bf16[2,512,128]{2,1,0:T(8,128)(2,1)} %param.12) | copy-start | bytes 786436
  76.8 61.2 %copy-start.7 = (bf16[2,4,128]{2,1,0:T(4,128)(2,1)S(1)}, bf16[2,4,128]{2,1,0:T(4,128)(2,1)}, u32[]{:S(2)}) copy-start(bf16[2,4,128]{2,1,0:T(4,128)(2,1)} %param.14) | copy-start | bytes 6148
  138.5 1.0 copy-start.2
  147.5 0.7 copy-start.3
  151.8 28.5 %all-to-all-start.4 = ((f32[1,4,32,16]{3,1,0,2:T(4,128)}), f32[1,4,32,16]{3,1,0,2:T(4,128)S(1)}, u32[]{:S(2)}, u32[]{:S(2)}) async-start(f32[1,4,32,16]{3,1,0,2:T(4,128)} %copy.58), calls=%async_computation.4 | async-start | bytes 131072 | tf_op jit(solution)/shard_map/all_to_all | solution.py:157
  180.3 28.5 %all-to-all-start.2 = ((f32[1,4,32,16]{3,1,0,2:T(4,128)}), f32[1,4,32,16]{3,1,0,2:T(4,128)S(1)}, u32[]{:S(2)}, u32[]{:S(2)}) async-start(f32[1,4,32,16]{3,1,0,2:T(4,128)} %copy.52), calls=%async_computation.2 | async-start | bytes 131072 | tf_op jit(solution)/shard_map/all_to_all | solution.py:156
  208.8 109.8 %all-to-all-start.3 = ((f32[1,4,32,16,128]{4,3,1,0,2:T(8,128)}), f32[1,4,32,16,128]{4,3,1,0,2:T(8,128)S(1)}, u32[]{:S(2)}, u32[]{:S(2)}) async-start(f32[1,4,32,16,128]{4,3,1,0,2:T(8,128)} %maximum_bitcast_fusion), calls=%async_computation.3 | async-start | bytes 2097152 | tf_op jit(solution)/shard_map/all_to_all | solution.py:158
  213.7 0.7 copy-start.8
